TPU v7x, 256 devices: a whole 4x4x8 slice. The times are simulated.
256 devices in a mesh: grp: 16 (over y_hi, x, core), sub: 16 (over y_lo, z).
Axes of the slice: x: 4, y: 4 (y_hi: 2, y_lo: 2; y = y_hi * 2 + y_lo), z: 8, core: 2. Of those that a mesh axis runs over, the one named last changes fastest.
Arguments:
- arrivals: float32 [128, 262144], P('sub', 'grp'), may hold values from -64 to 64
- sketch: float32 [256, 262144], P(None, ('grp', 'sub')), may hold values from -96 to 96
- owner: int32 [8192], P('grp'), may hold values from 0 to 511, as said below
- slot: int32 [128], replicated, may hold values from 0 to 127, each once
Outputs:
- final_sketch: float32 [256, 262144], P(None, ('grp', 'sub'))
- residual: float32 [128, 262144], P(None, ('grp', 'sub'))
Inputs may be any that keep to these rules, and one draw needn't show every extreme that they name: `owner`: each aligned block of 512 entries names each host of its group once. `slot`: each time step has its own arrival row.
All inputs are finite; a program needn't handle non-finite values.
Results may differ from a plain program's by a relative error of at most 0.00016.
Values sent between devices are 32-bit elements; how exact they have to be, the bound alone decides.
A program may use at most 64 MiB of HBM per device.

v0:
```python
import jax
import jax.numpy as jnp
from jax import lax
from jax.sharding import Mesh
from jax.sharding import PartitionSpec as P

ELL = 256
NEW = 64
TOP = 32
ROWS = 320
SUB = ("sub_0", "sub_1")
GRP_SUB = ("grp_0", "grp_1", "grp_2", "sub_0", "sub_1")
GRP = ("grp_0", "grp_1", "grp_2")
highest = lax.Precision.HIGHEST


def one_axis_at_a_time(x, axes):
    for axis in axes:
        x = lax.psum(x, axis)
    return x


def product(former, latter):
    return jnp.dot(former, latter, precision=highest, preferred_element_type=jnp.float32)


def symmetric(matrix):
    return 0.5 * (matrix + matrix.T)


def lower_inverse(triangle):
    identity = jnp.eye(triangle.shape[0], dtype=jnp.float32)
    return jax.scipy.linalg.solve_triangular(triangle, identity, lower=True)


def orthonormal(columns):
    factor = jnp.linalg.cholesky(symmetric(product(columns.T, columns)))
    return jax.scipy.linalg.solve_triangular(factor, columns.T, lower=True).T


def shrink_factors(gram_matrix):
    subspace = orthonormal(gram_matrix[:, :ELL])
    reduced = symmetric(product(subspace.T, product(gram_matrix, subspace)))
    inverse_root = lower_inverse(jnp.linalg.cholesky(reduced))
    offset = 0.5 / jnp.sum(inverse_root * inverse_root)
    keeper = jnp.eye(ELL, dtype=jnp.float32) - offset * product(inverse_root.T, inverse_root)
    shrink_factor = jnp.linalg.cholesky(symmetric(keeper)).T
    return (product(shrink_factor, subspace.T), shrink_factor, reduced)


def local(arrivals, sketch, owner, slot):
    arrived_rows, arrived_columns = arrivals.shape
    host_count = owner.shape[0]
    shaped = arrivals.reshape(arrived_rows, host_count, arrived_columns // host_count)
    placed = jnp.take(shaped, owner, axis=1).reshape(arrived_rows, arrived_columns)
    regrouped = lax.all_to_all(placed, SUB, split_axis=1, concat_axis=0, tiled=True)
    samples = jnp.take(regrouped, slot, axis=0)
    first_batch = samples[:NEW]
    second_batch = samples[NEW:]
    stacked = jnp.concatenate([sketch, first_batch], axis=0)
    gram_one = lax.psum(product(stacked, stacked.T), GRP_SUB)
    weights_one, factor_one, reduced_one = shrink_factors(gram_one)
    middle = product(weights_one, stacked)
    stacked_two = jnp.concatenate([middle, second_batch], axis=0)
    extended = jnp.concatenate([stacked_two, first_batch], axis=0)
    summed = one_axis_at_a_time(product(extended, second_batch.T), GRP_SUB)
    corner = symmetric(product(factor_one, product(reduced_one, factor_one.T)))
    side_block = summed[:ROWS]
    upper_rows = jnp.concatenate([corner, side_block[:ELL]], axis=1)
    gram_two = jnp.concatenate([upper_rows, side_block.T], axis=0)
    early_rows = jnp.concatenate([product(gram_one[ELL:], weights_one.T), summed[ROWS:]], axis=1)
    weights_two, factor_two, reduced_two = shrink_factors(gram_two)
    final_sketch = product(weights_two, stacked_two)
    spectrum = symmetric(product(factor_two, product(reduced_two, factor_two.T)))
    leading = orthonormal(spectrum[:, :TOP])
    directions = product(leading.T, final_sketch)
    small_gram = symmetric(product(leading.T, product(spectrum, leading)))
    inverse_root = lower_inverse(jnp.linalg.cholesky(small_gram))
    sample_rows = jnp.concatenate([early_rows, gram_two[ELL:]], axis=0)
    scores = product(sample_rows, product(weights_two.T, leading))
    coefficients = product(product(scores, inverse_root.T), inverse_root)
    residual = samples - product(coefficients, directions)
    return (final_sketch, residual)


def solution(mesh):
    split = Mesh(mesh.devices.reshape(2, 4, 2, 2, 8), ("grp_0", "grp_1", "grp_2", "sub_0", "sub_1"))
    placed = (P(SUB, GRP), P(None, GRP_SUB), P(GRP), P())
    return jax.shard_map(
        local,
        mesh=split,
        in_specs=placed,
        out_specs=(P(None, GRP_SUB), P(None, GRP_SUB)),
        check_vma=False,
    )
```

profile of v0, /device:TPU:2, one launch (start us, length us, event | category | flops | bytes accessed | tf_op | source)
XLA Modules:
  0.0 899.6 jit_solution(13229806428466531764)
XLA Ops:
  8.5 1.7 reshape.63
  10.3 2.6 copy.53
  12.8 3.9 gather_fusion
  16.7 2.0 copy.54
  21.2 9.6 %all-to-all-start = ((f32[8,16,1024]{2,0,1:T(8,128)}), f32[8,16,1024]{2,0,1:T(8,128)S(1)}, u32[]{:S(2)}, u32[]{:S(2)}) async-start(f32[8,16,1024]{2,0,1:T(8,128)} %copy.55), calls=%async_computation | async-start | bytes 1048576 | tf_op jit(solution)/shard_map/all_to_all | solution.py:56
  31.1 15.4 %all-to-all-done = f32[8,16,1024]{2,0,1:T(8,128)S(1)} async-done(((f32[8,16,1024]{2,0,1:T(8,128)}), f32[8,16,1024]{2,0,1:T(8,128)S(1)}, u32[]{:S(2)}, u32[]{:S(2)}) %all-to-all-start) | async-done | bytes 524320 | tf_op jit(solution)/shard_map/all_to_all | solution.py:56
  48.6 3.0 fusion.11
  52.0 253.9 %all-reduce.8.cloned.1.call-done = f32[320,320]{1,0:T(8,128)} async-done(((f32[320,320]{1,0:T(8,128)}), f32[320,320]{1,0:T(8,128)}) %all-reduce.8.cloned.1.call-update) | async-done | bytes 409616 | tf_op jit(solution)/shard_map/psum | solution.py:61
  305.9 2.0 fusion.18
  308.2 11.7 %cholesky.340 = f32[128,128]{1,0:T(8,128)S(1)} custom-call(f32[128,128]{1,0:T(8,128)S(1)} %cholesky.562), custom_call_target="Cholesky" | custom-call | tf_op jit(solution)/shard_map/jit(cholesky)/cholesky | solution.py:37
  320.0 9.8 %custom-call.33 = f32[1,128,128]{1,2,0:T(8,128)S(1)} custom-call(f32[1,128,128]{2,1,0:T(8,128)S(1)} %get-tuple-element.103), custom_call_target="InvertDiagBlocksLowerTriangular" | custom-call | tf_op jit(solution)/shard_map/jit(cholesky)/cholesky | solution.py:37
  330.3 11.7 %cholesky.357 = f32[128,128]{1,0:T(8,128)S(1)} custom-call(f32[128,128]{1,0:T(8,128)S(1)} %convolution_subtract_fusion.10), custom_call_target="Cholesky" | custom-call | tf_op jit(solution)/shard_map/jit(cholesky)/cholesky | solution.py:37
  344.0 3.8 while.8
  347.9 20.1 %custom-call.34 = f32[2,128,128]{1,2,0:T(8,128)S(1)} custom-call(f32[2,128,128]{2,1,0:T(8,128)S(1)} %get-tuple-element.34), custom_call_target="InvertDiagBlocksLowerTriangular" | custom-call | tf_op jit(solution)/shard_map/jit(_solve_triangular)/triangular_solve | solution.py:38
  370.9 11.7 %cholesky.374 = f32[128,128]{1,0:T(8,128)S(1)} custom-call(f32[128,128]{1,0:T(8,128)S(1)} %cholesky.565), custom_call_target="Cholesky" | custom-call | tf_op jit(solution)/shard_map/jit(cholesky)/cholesky | solution.py:44
  382.6 9.8 %custom-call.35 = f32[1,128,128]{1,2,0:T(8,128)S(1)} custom-call(f32[1,128,128]{2,1,0:T(8,128)S(1)} %get-tuple-element.99), custom_call_target="InvertDiagBlocksLowerTriangular" | custom-call | tf_op jit(solution)/shard_map/jit(cholesky)/cholesky | solution.py:44
  392.9 11.9 %cholesky.391 = f32[128,128]{1,0:T(8,128)S(1)} custom-call(f32[128,128]{1,0:T(8,128)S(1)} %convolution_subtract_fusion.9), custom_call_target="Cholesky" | custom-call | tf_op jit(solution)/shard_map/jit(cholesky)/cholesky | solution.py:44
  407.6 4.1 while.9
  411.7 19.7 %custom-call.36 = f32[2,128,128]{1,2,0:T(8,128)S(1)} custom-call(f32[2,128,128]{2,1,0:T(8,128)S(1)} %get-tuple-element.35), custom_call_target="InvertDiagBlocksLowerTriangular" | custom-call | tf_op jit(solution)/shard_map/jit(_solve_triangular)/triangular_solve | solution.py:33
  434.7 11.7 %cholesky.408 = f32[128,128]{1,0:T(8,128)S(1)} custom-call(f32[128,128]{1,0:T(8,128)S(1)} %cholesky.568), custom_call_target="Cholesky" | custom-call | tf_op jit(solution)/shard_map/jit(cholesky)/cholesky | solution.py:47
  446.4 9.8 %custom-call.37 = f32[1,128,128]{1,2,0:T(8,128)S(1)} custom-call(f32[1,128,128]{2,1,0:T(8,128)S(1)} %get-tuple-element.95), custom_call_target="InvertDiagBlocksLowerTriangular" | custom-call | tf_op jit(solution)/shard_map/jit(cholesky)/cholesky | solution.py:47
  456.7 11.7 %cholesky.425 = f32[128,128]{1,0:T(8,128)S(1)} custom-call(f32[128,128]{1,0:T(8,128)S(1)} %convolution_subtract_fusion.8), custom_call_target="Cholesky" | custom-call | tf_op jit(solution)/shard_map/jit(cholesky)/cholesky | solution.py:47
  472.1 2.8 fusion.10
  475.0 2.3 fusion
  477.3 31.7 %all-reduce.10.cloned.1.call-done = f32[384,64]{0,1:T(8,128)} async-done(((f32[384,64]{0,1:T(8,128)}), f32[384,64]{0,1:T(8,128)}) %all-reduce.10.cloned.1.call-update) | async-done | bytes 98320 | tf_op jit(solution)/shard_map/psum | solution.py:19
  509.7 46.3 %all-reduce.12.cloned.1.call-done = f32[384,64]{0,1:T(8,128)} async-done(((f32[384,64]{0,1:T(8,128)}), f32[384,64]{0,1:T(8,128)}) %all-reduce.12.cloned.1.call-update) | async-done | bytes 98320 | tf_op jit(solution)/shard_map/psum | solution.py:19
  556.8 32.0 %all-reduce.14.cloned.1.call-done = f32[384,64]{0,1:T(8,128)} async-done(((f32[384,64]{0,1:T(8,128)}), f32[384,64]{0,1:T(8,128)}) %all-reduce.14.cloned.1.call-update) | async-done | bytes 98320 | tf_op jit(solution)/shard_map/psum | solution.py:19
  588.9 36.5 %all-reduce.16.cloned.1.call-done = f32[384,64]{0,1:T(8,128)} async-done(((f32[384,64]{0,1:T(8,128)}), f32[384,64]{0,1:T(8,128)}) %all-reduce.16.cloned.1.call-update) | async-done | bytes 98320 | tf_op jit(solution)/shard_map/psum | solution.py:19
  625.4 2.4 fusion.85
  627.8 73.3 %all-reduce.18.cloned.1.call-done = f32[384,64]{0,1:T(8,128)} async-done(((f32[384,64]{0,1:T(8,128)}), f32[384,64]{0,1:T(8,128)}) %all-reduce.18.cloned.1.call-update) | async-done | bytes 98320 | tf_op jit(solution)/shard_map/psum | solution.py:19
  703.9 11.7 %cholesky.442 = f32[128,128]{1,0:T(8,128)S(1)} custom-call(f32[128,128]{1,0:T(8,128)S(1)} %cholesky.571), custom_call_target="Cholesky" | custom-call | tf_op jit(solution)/shard_map/jit(cholesky)/cholesky | solution.py:37
  715.7 9.8 %custom-call.38 = f32[1,128,128]{1,2,0:T(8,128)S(1)} custom-call(f32[1,128,128]{2,1,0:T(8,128)S(1)} %get-tuple-element.91), custom_call_target="InvertDiagBlocksLowerTriangular" | custom-call | tf_op jit(solution)/shard_map/jit(cholesky)/cholesky | solution.py:37
  726.0 11.7 %cholesky.459 = f32[128,128]{1,0:T(8,128)S(1)} custom-call(f32[128,128]{1,0:T(8,128)S(1)} %convolution_subtract_fusion.7), custom_call_target="Cholesky" | custom-call | tf_op jit(solution)/shard_map/jit(cholesky)/cholesky | solution.py:37
  740.5 4.1 while.10
  744.6 19.8 %custom-call.39 = f32[2,128,128]{1,2,0:T(8,128)S(1)} custom-call(f32[2,128,128]{2,1,0:T(8,128)S(1)} %get-tuple-element.36), custom_call_target="InvertDiagBlocksLowerTriangular" | custom-call | tf_op jit(solution)/shard_map/jit(_solve_triangular)/triangular_solve | solution.py:38
  768.1 11.7 %cholesky.476 = f32[128,128]{1,0:T(8,128)S(1)} custom-call(f32[128,128]{1,0:T(8,128)S(1)} %cholesky.574), custom_call_target="Cholesky" | custom-call | tf_op jit(solution)/shard_map/jit(cholesky)/cholesky | solution.py:44
  779.8 9.8 %custom-call.40 = f32[1,128,128]{1,2,0:T(8,128)S(1)} custom-call(f32[1,128,128]{2,1,0:T(8,128)S(1)} %get-tuple-element.87), custom_call_target="InvertDiagBlocksLowerTriangular" | custom-call | tf_op jit(solution)/shard_map/jit(cholesky)/cholesky | solution.py:44
  790.1 11.9 %cholesky.493 = f32[128,128]{1,0:T(8,128)S(1)} custom-call(f32[128,128]{1,0:T(8,128)S(1)} %convolution_subtract_fusion.6), custom_call_target="Cholesky" | custom-call | tf_op jit(solution)/shard_map/jit(cholesky)/cholesky | solution.py:44
  804.7 4.0 while.11
  808.7 19.7 %custom-call.41 = f32[2,128,128]{1,2,0:T(8,128)S(1)} custom-call(f32[2,128,128]{2,1,0:T(8,128)S(1)} %get-tuple-element.37), custom_call_target="InvertDiagBlocksLowerTriangular" | custom-call | tf_op jit(solution)/shard_map/jit(_solve_triangular)/triangular_solve | solution.py:33
  831.9 11.7 %cholesky.510 = f32[128,128]{1,0:T(8,128)S(1)} custom-call(f32[128,128]{1,0:T(8,128)S(1)} %cholesky.577), custom_call_target="Cholesky" | custom-call | tf_op jit(solution)/shard_map/jit(cholesky)/cholesky | solution.py:47
  843.7 9.8 %custom-call.42 = f32[1,128,128]{1,2,0:T(8,128)S(1)} custom-call(f32[1,128,128]{2,1,0:T(8,128)S(1)} %get-tuple-element.83), custom_call_target="InvertDiagBlocksLowerTriangular" | custom-call | tf_op jit(solution)/shard_map/jit(cholesky)/cholesky | solution.py:47
  854.0 11.7 %cholesky.527 = f32[128,128]{1,0:T(8,128)S(1)} custom-call(f32[128,128]{1,0:T(8,128)S(1)} %convolution_subtract_fusion.5), custom_call_target="Cholesky" | custom-call | tf_op jit(solution)/shard_map/jit(cholesky)/cholesky | solution.py:47
  870.7 2.9 cholesky.542
  875.1 2.4 custom-call.24
  877.8 2.8 fusion.6
  882.3 2.9 cholesky.553
  886.7 2.4 custom-call.25
  (218 shorter events, 60.6 us)
Async XLA Ops:
  20.1 10.9 %copy-start.9 = (s32[128]{0:T(128)S(1)}, s32[128]{0:T(128)}, u32[]{:S(2)}) copy-start(s32[128]{0:T(128)} %param.13) | copy-start | bytes 1540
  21.2 25.3 %all-to-all-start = ((f32[8,16,1024]{2,0,1:T(8,128)}), f32[8,16,1024]{2,0,1:T(8,128)S(1)}, u32[]{:S(2)}, u32[]{:S(2)}) async-start(f32[8,16,1024]{2,0,1:T(8,128)} %copy.55), calls=%async_computation | async-start | bytes 1048576 | tf_op jit(solution)/shard_map/all_to_all | solution.py:56
  30.8 275.0 %all-reduce.8.cloned.1.call-start = ((), (), s32[]{:S(2)}) async-start(), calls=%async_computation.1 | async-start | bytes 983040 | tf_op jit(solution)/shard_map/psum | solution.py:61
  47.3 1.3 copy-start
  48.2 259.7 %copy-start.5 = (f32[64,1024]{1,0:T(8,128)}, f32[64,1024]{1,0:T(8,128)S(1)}, u32[]{:S(2)}) copy-start(f32[64,1024]{1,0:T(8,128)S(1)} %get-tuple-element.78) | copy-start | bytes 786436
  51.7 457.4 %all-reduce.10.cloned.1.call-start = ((), (), s32[]{:S(2)}) async-start(), calls=%async_computation.2 | async-start | bytes 196608 | tf_op jit(solution)/shard_map/psum | solution.py:19
  52.0 379.7 %copy-start.3 = (f32[256,256]{1,0:T(8,128)}, f32[256,256]{1,0:T(8,128)S(1)}, u32[]{:S(2)}) copy-start(f32[256,256]{1,0:T(8,128)S(1)} %fusion.36) | copy-start | bytes 786436
  308.2 59.8 %copy-start.2 = (f32[320,320]{1,0:T(8,128)S(1)}, f32[320,320]{1,0:T(8,128)}, u32[]{:S(2)}) copy-start(f32[320,320]{1,0:T(8,128)} %all-reduce.8.cloned.1.call-done) | copy-start | bytes 1228804
  472.1 2.9 copy-start.6
  472.1 2.9 copy-start.7
  477.2 78.8 %all-reduce.12.cloned.1.call-start = ((), (), s32[]{:S(2)}) async-start(), calls=%async_computation.3 | async-start | bytes 196608 | tf_op jit(solution)/shard_map/psum | solution.py:19
  509.1 79.7 %all-reduce.14.cloned.1.call-start = ((), (), s32[]{:S(2)}) async-start(), calls=%async_computation.4 | async-start | bytes 196608 | tf_op jit(solution)/shard_map/psum | solution.py:19
  556.1 69.3 %all-reduce.16.cloned.1.call-start = ((), (), s32[]{:S(2)}) async-start(), calls=%async_computation.5 | async-start | bytes 196608 | tf_op jit(solution)/shard_map/psum | solution.py:19
  588.8 112.2 %all-reduce.18.cloned.1.call-start = ((), (), s32[]{:S(2)}) async-start(), calls=%async_computation.6 | async-start | bytes 196608 | tf_op jit(solution)/shard_map/psum | solution.py:19
  768.0 60.4 %copy-start.4 = (f32[256,256]{1,0:T(8,128)S(1)}, f32[256,256]{1,0:T(8,128)}, u32[]{:S(2)}) copy-start(f32[256,256]{1,0:T(8,128)} %copy-done.3) | copy-start | bytes 786436
  880.6 11.7 %copy-start.1 = (f32[256,1024]{1,0:T(8,128)}, f32[256,1024]{1,0:T(8,128)S(1)}, u32[]{:S(2)}) copy-start(f32[256,1024]{1,0:T(8,128)S(1)} %fusion.6) | copy-start | bytes 3145732
  880.6 9.6 %copy-start.8 = (f32[64,256]{0,1:T(8,128)S(1)}, f32[64,256]{0,1:T(8,128)}, u32[]{:S(2)}) copy-start(f32[64,256]{0,1:T(8,128)} %fusion.85) | copy-start | bytes 196612
Sparse Core Ops, SparseCore 0:
  51.8 254.0 all-reduce.7
  477.4 31.6 all-reduce.9
  511.4 44.6 all-reduce.11
  558.5 30.2 all-reduce.13
  591.1 34.1 all-reduce.15
  627.6 73.4 all-reduce.17
where the time goes:
time: 906 us; the launch traced here: 900 us
  waiting for transfers between devices  489 us (54%)
  other arithmetic  304 us (34%)
  local copies, waits for them, and re-layouts  35.8 us (4%)
  matrix products  35.2 us (4%)
  between operations  24.8 us (3%)
  starting transfers between devices  10 us (1%)
    psum x1, waiting for transfers between devices, local(): gram_one = lax.psum(product(stacked, stacked.T), GRP_SUB)  254 us
    psum x5, waiting for transfers between devices, one_axis_at_a_time(): x = lax.psum(x, axis)  220 us
    another operation x16, other arithmetic, orthonormal(): factor = jnp.linalg.cholesky(symmetric(product(columns.T, columns)))  72.3 us
    another operation x14, other arithmetic, shrink_factors(): inverse_root = lower_inverse(jnp.linalg.cholesky(reduced))  69.7 us
    another operation x14, other arithmetic, shrink_factors(): shrink_factor = jnp.linalg.cholesky(symmetric(keeper)).T  69.3 us
    another operation x7, other arithmetic, orthonormal(): return jax.scipy.linalg.solve_triangular(factor, columns.T, lower=True).T  43.2 us
    another operation x6, other arithmetic, lower_inverse(): return jax.scipy.linalg.solve_triangular(triangle, identity, lower=True)  42.5 us
    dot_general x28, matrix products, product(): jnp.dot(former, latter, precision=highest, preferred_element_type=jnp.flo...  28 us
  transfers between devices with their start and end apart: 7, of which 7 were waited for; matrix products, arithmetic and copies ran while one was open for 0% of the time, Pallas kernels for 0%

commit v1 on v0

--- a/solution.py
+++ b/solution.py
@@ -16,7 +16,7 @@
 
 def one_axis_at_a_time(x, axes):
     for axis in axes:
-        x = lax.psum(x, axis)
+        x = jnp.sum(lax.all_gather(x, axis), axis=0)
     return x
 
 

time: 906 us -> 767 us (0.85)
  waiting for transfers between devices: 489 us -> 269 us
  blocking collectives: 0 us -> 53.6 us
  matrix products: 35.2 us -> 48.3 us
  other arithmetic: 304 us -> 314 us
    psum x5 -> x0, waiting for transfers between devices: 220 us -> none  [one_axis_at_a_time(): x = lax.psum(x, axis)]
    all_gather x0 -> x5, blocking collectives: none -> 53.6 us  [one_axis_at_a_time(): x = jnp.sum(lax.all_gather(x, axis), axis=0)]
  transfers between devices with their start and end apart: 7 -> 2, of which waited for: 7 -> 2; matrix products, arithmetic and copies ran while one was open for 0% -> 0% of each run, Pallas kernels for 0% -> 0%
where the time goes in v1:
time: 767 us; the launch traced here: 761 us
  other arithmetic  314 us (41%)
  waiting for transfers between devices  269 us (35%)
  blocking collectives  53.6 us (7%)
  matrix products  48.3 us (6%)
  local copies, waits for them, and re-layouts  42.2 us (6%)
  between operations  24.6 us (3%)
  starting transfers between devices  9.84 us (1%)
    psum x1, waiting for transfers between devices, local(): gram_one = lax.psum(product(stacked, stacked.T), GRP_SUB)  254 us
    another operation x16, other arithmetic, orthonormal(): factor = jnp.linalg.cholesky(symmetric(product(columns.T, columns)))  72.8 us
    another operation x14, other arithmetic, shrink_factors(): inverse_root = lower_inverse(jnp.linalg.cholesky(reduced))  69.6 us
    another operation x14, other arithmetic, shrink_factors(): shrink_factor = jnp.linalg.cholesky(symmetric(keeper)).T  69.2 us
    all_gather x5, blocking collectives, one_axis_at_a_time(): x = jnp.sum(lax.all_gather(x, axis), axis=0)  53.6 us
    another operation x6, other arithmetic, lower_inverse(): return jax.scipy.linalg.solve_triangular(triangle, identity, lower=True)  45 us
    another operation x7, other arithmetic, orthonormal(): return jax.scipy.linalg.solve_triangular(factor, columns.T, lower=True).T  44.3 us
    dot_general x28, matrix products, product(): jnp.dot(former, latter, precision=highest, preferred_element_type=jnp.flo...  29.4 us
  transfers between devices with their start and end apart: 2, of which 2 were waited for; matrix products, arithmetic and copies ran while one was open for 0% of the time, Pallas kernels for 0%

profile of v1, /device:TPU:2, one launch (start us, length us, event | category | flops | bytes accessed | tf_op | source)
XLA Modules:
  0.0 761.1 jit_solution(12705334473970715213)
XLA Ops:
  8.5 1.7 reshape.63
  10.3 2.6 copy.134
  12.8 3.9 gather_fusion
  16.7 2.0 copy.135
  21.2 9.6 %all-to-all-start = ((f32[8,16,1024]{2,0,1:T(8,128)}), f32[8,16,1024]{2,0,1:T(8,128)S(1)}, u32[]{:S(2)}, u32[]{:S(2)}) async-start(f32[8,16,1024]{2,0,1:T(8,128)} %copy.136), calls=%async_computation | async-start | bytes 1048576 | tf_op jit(solution)/shard_map/all_to_all | solution.py:56
  32.0 14.5 %all-to-all-done = f32[8,16,1024]{2,0,1:T(8,128)S(1)} async-done(((f32[8,16,1024]{2,0,1:T(8,128)}), f32[8,16,1024]{2,0,1:T(8,128)S(1)}, u32[]{:S(2)}, u32[]{:S(2)}) %all-to-all-start) | async-done | bytes 524320 | tf_op jit(solution)/shard_map/all_to_all | solution.py:56
  48.6 3.0 fusion.11
  51.7 254.1 %all-reduce.3.cloned.1.call-done = f32[320,320]{1,0:T(8,128)} async-done(((f32[320,320]{1,0:T(8,128)}), f32[320,320]{1,0:T(8,128)}) %all-reduce.3.cloned.1.call-update) | async-done | bytes 409616 | tf_op jit(solution)/shard_map/psum | solution.py:61
  305.8 2.0 fusion.18
  308.2 11.7 %cholesky.340 = f32[128,128]{1,0:T(8,128)S(1)} custom-call(f32[128,128]{1,0:T(8,128)S(1)} %cholesky.562), custom_call_target="Cholesky" | custom-call | tf_op jit(solution)/shard_map/jit(cholesky)/cholesky | solution.py:37
  320.0 9.8 %custom-call.33 = f32[1,128,128]{1,2,0:T(8,128)S(1)} custom-call(f32[1,128,128]{2,1,0:T(8,128)S(1)} %get-tuple-element.103), custom_call_target="InvertDiagBlocksLowerTriangular" | custom-call | tf_op jit(solution)/shard_map/jit(cholesky)/cholesky | solution.py:37
  330.3 12.2 %cholesky.357 = f32[128,128]{1,0:T(8,128)S(1)} custom-call(f32[128,128]{1,0:T(8,128)S(1)} %convolution_subtract_fusion.10), custom_call_target="Cholesky" | custom-call | tf_op jit(solution)/shard_map/jit(cholesky)/cholesky | solution.py:37
  344.7 4.1 while.8
  348.7 19.7 %custom-call.34 = f32[2,128,128]{1,2,0:T(8,128)S(1)} custom-call(f32[2,128,128]{2,1,0:T(8,128)S(1)} %get-tuple-element.34), custom_call_target="InvertDiagBlocksLowerTriangular" | custom-call | tf_op jit(solution)/shard_map/jit(_solve_triangular)/triangular_solve | solution.py:38
  373.6 11.7 %cholesky.374 = f32[128,128]{1,0:T(8,128)S(1)} custom-call(f32[128,128]{1,0:T(8,128)S(1)} %cholesky.565), custom_call_target="Cholesky" | custom-call | tf_op jit(solution)/shard_map/jit(cholesky)/cholesky | solution.py:44
  385.4 9.8 %custom-call.35 = f32[1,128,128]{1,2,0:T(8,128)S(1)} custom-call(f32[1,128,128]{2,1,0:T(8,128)S(1)} %get-tuple-element.99), custom_call_target="InvertDiagBlocksLowerTriangular" | custom-call | tf_op jit(solution)/shard_map/jit(cholesky)/cholesky | solution.py:44
  397.4 11.9 %cholesky.391 = f32[128,128]{1,0:T(8,128)S(1)} custom-call(f32[128,128]{1,0:T(8,128)S(1)} %convolution_subtract_fusion.9), custom_call_target="Cholesky" | custom-call | tf_op jit(solution)/shard_map/jit(cholesky)/cholesky | solution.py:44
  412.9 4.1 while.9
  417.0 19.7 %custom-call.36 = f32[2,128,128]{1,2,0:T(8,128)S(1)} custom-call(f32[2,128,128]{2,1,0:T(8,128)S(1)} %get-tuple-element.35), custom_call_target="InvertDiagBlocksLowerTriangular" | custom-call | tf_op jit(solution)/shard_map/jit(_solve_triangular)/triangular_solve | solution.py:33
  443.1 11.7 %cholesky.408 = f32[128,128]{1,0:T(8,128)S(1)} custom-call(f32[128,128]{1,0:T(8,128)S(1)} %cholesky.568), custom_call_target="Cholesky" | custom-call | tf_op jit(solution)/shard_map/jit(cholesky)/cholesky | solution.py:47
  454.9 9.8 %custom-call.37 = f32[1,128,128]{1,2,0:T(8,128)S(1)} custom-call(f32[1,128,128]{2,1,0:T(8,128)S(1)} %get-tuple-element.95), custom_call_target="InvertDiagBlocksLowerTriangular" | custom-call | tf_op jit(solution)/shard_map/jit(cholesky)/cholesky | solution.py:47
  466.9 11.7 %cholesky.425 = f32[128,128]{1,0:T(8,128)S(1)} custom-call(f32[128,128]{1,0:T(8,128)S(1)} %convolution_subtract_fusion.8), custom_call_target="Cholesky" | custom-call | tf_op jit(solution)/shard_map/jit(cholesky)/cholesky | solution.py:47
  484.0 2.9 fusion.10
  487.0 1.6 fusion
  488.6 6.8 all-gather
  495.7 13.0 %all-gather.1 = f32[1536,64]{0,1:T(8,128)S(1)} all-gather(f32[384,64]{0,1:T(8,128)S(1)} %reduce_sum.64), channel_id=3, replica_groups=mesh['grp_0'=2,'grp_1'=4,'grp_2'=2,'sub_0'=2,'sub_1'=8] {'grp_1'}, dimensions={0}, use_global_device_ids=true | all-gather | bytes 491520 | tf_op jit(solution)/shard_map/all_gather | solution.py:19
  509.1 1.9 all-gather.2
  511.4 5.5 all-gather.3
  517.3 26.3 %all-gather.4 = f32[3072,64]{0,1:T(8,128)S(1)} all-gather(f32[384,64]{0,1:T(8,128)S(1)} %reduce_sum.67), channel_id=6, replica_groups=mesh['grp_0'=2,'grp_1'=4,'grp_2'=2,'sub_0'=2,'sub_1'=8] {'sub_1'}, dimensions={0}, use_global_device_ids=true | all-gather | bytes 884736 | tf_op jit(solution)/shard_map/all_gather | solution.py:19
  546.5 11.7 %cholesky.442 = f32[128,128]{1,0:T(8,128)S(1)} custom-call(f32[128,128]{1,0:T(8,128)S(1)} %cholesky.571), custom_call_target="Cholesky" | custom-call | tf_op jit(solution)/shard_map/jit(cholesky)/cholesky | solution.py:37
  558.3 9.8 %custom-call.38 = f32[1,128,128]{1,2,0:T(8,128)S(1)} custom-call(f32[1,128,128]{2,1,0:T(8,128)S(1)} %get-tuple-element.91), custom_call_target="InvertDiagBlocksLowerTriangular" | custom-call | tf_op jit(solution)/shard_map/jit(cholesky)/cholesky | solution.py:37
  570.3 11.7 %cholesky.459 = f32[128,128]{1,0:T(8,128)S(1)} custom-call(f32[128,128]{1,0:T(8,128)S(1)} %convolution_subtract_fusion.7), custom_call_target="Cholesky" | custom-call | tf_op jit(solution)/shard_map/jit(cholesky)/cholesky | solution.py:37
  585.7 4.1 while.10
  589.7 20.4 %custom-call.39 = f32[2,128,128]{1,2,0:T(8,128)} custom-call(f32[2,128,128]{2,1,0:T(8,128)S(1)} %get-tuple-element.36), custom_call_target="InvertDiagBlocksLowerTriangular" | custom-call | tf_op jit(solution)/shard_map/jit(_solve_triangular)/triangular_solve | solution.py:38
  616.2 11.7 %cholesky.476 = f32[128,128]{1,0:T(8,128)S(1)} custom-call(f32[128,128]{1,0:T(8,128)S(1)} %cholesky.574), custom_call_target="Cholesky" | custom-call | tf_op jit(solution)/shard_map/jit(cholesky)/cholesky | solution.py:44
  628.0 9.8 %custom-call.40 = f32[1,128,128]{1,2,0:T(8,128)S(1)} custom-call(f32[1,128,128]{2,1,0:T(8,128)S(1)} %get-tuple-element.87), custom_call_target="InvertDiagBlocksLowerTriangular" | custom-call | tf_op jit(solution)/shard_map/jit(cholesky)/cholesky | solution.py:44
  639.9 11.9 %cholesky.493 = f32[128,128]{1,0:T(8,128)S(1)} custom-call(f32[128,128]{1,0:T(8,128)S(1)} %convolution_subtract_fusion.6), custom_call_target="Cholesky" | custom-call | tf_op jit(solution)/shard_map/jit(cholesky)/cholesky | solution.py:44
  655.5 4.1 while.11
  659.6 20.3 %custom-call.41 = f32[2,128,128]{1,2,0:T(8,128)} custom-call(f32[2,128,128]{2,1,0:T(8,128)S(1)} %get-tuple-element.37), custom_call_target="InvertDiagBlocksLowerTriangular" | custom-call | tf_op jit(solution)/shard_map/jit(_solve_triangular)/triangular_solve | solution.py:33
  689.0 11.7 %cholesky.510 = f32[128,128]{1,0:T(8,128)S(1)} custom-call(f32[128,128]{1,0:T(8,128)S(1)} %cholesky.577), custom_call_target="Cholesky" | custom-call | tf_op jit(solution)/shard_map/jit(cholesky)/cholesky | solution.py:47
  700.8 9.8 %custom-call.42 = f32[1,128,128]{1,2,0:T(8,128)S(1)} custom-call(f32[1,128,128]{2,1,0:T(8,128)S(1)} %get-tuple-element.83), custom_call_target="InvertDiagBlocksLowerTriangular" | custom-call | tf_op jit(solution)/shard_map/jit(cholesky)/cholesky | solution.py:47
  712.8 11.7 %cholesky.527 = f32[128,128]{1,0:T(8,128)S(1)} custom-call(f32[128,128]{1,0:T(8,128)S(1)} %convolution_subtract_fusion.5), custom_call_target="Cholesky" | custom-call | tf_op jit(solution)/shard_map/jit(cholesky)/cholesky | solution.py:47
  730.3 2.9 cholesky.542
  734.6 2.4 custom-call.24
  737.3 2.9 fusion.6
  740.5 1.6 fusion.177
  744.0 2.9 cholesky.553
  748.2 2.4 custom-call.25
  (238 shorter events, 89.3 us)
Async XLA Ops:
  20.1 11.8 %copy-start.19 = (s32[128]{0:T(128)S(1)}, s32[128]{0:T(128)}, u32[]{:S(2)}) copy-start(s32[128]{0:T(128)} %param.13) | copy-start | bytes 1540
  21.2 25.3 %all-to-all-start = ((f32[8,16,1024]{2,0,1:T(8,128)}), f32[8,16,1024]{2,0,1:T(8,128)S(1)}, u32[]{:S(2)}, u32[]{:S(2)}) async-start(f32[8,16,1024]{2,0,1:T(8,128)} %copy.136), calls=%async_computation | async-start | bytes 1048576 | tf_op jit(solution)/shard_map/all_to_all | solution.py:56
  30.8 275.0 %all-reduce.3.cloned.1.call-start = ((), (), s32[]{:S(2)}) async-start(), calls=%async_computation.1 | async-start | bytes 983040 | tf_op jit(solution)/shard_map/psum | solution.py:61
  47.3 1.3 copy-start
  48.2 259.7 %copy-start.6 = (f32[64,1024]{1,0:T(8,128)}, f32[64,1024]{1,0:T(8,128)S(1)}, u32[]{:S(2)}) copy-start(f32[64,1024]{1,0:T(8,128)S(1)} %get-tuple-element.78) | copy-start | bytes 786436
  51.7 385.3 %copy-start.4 = (f32[256,256]{1,0:T(8,128)}, f32[256,256]{1,0:T(8,128)S(1)}, u32[]{:S(2)}) copy-start(f32[256,256]{1,0:T(8,128)S(1)} %fusion.36) | copy-start | bytes 786436
  308.2 60.2 %copy-start.2 = (f32[320,320]{1,0:T(8,128)S(1)}, f32[320,320]{1,0:T(8,128)}, u32[]{:S(2)}) copy-start(f32[320,320]{1,0:T(8,128)} %all-reduce.3.cloned.1.call-done) | copy-start | bytes 1228804
  372.9 0.7 copy-start.17
  409.3 2.6 copy-start.9
  442.4 0.7 copy-start.15
  483.9 3.0 copy-start.7
  483.9 3.0 copy-start.12
  543.9 1.5 copy-start.13
  545.8 0.7 copy-start.16
  546.5 63.6 %copy-start.8 = (f32[256,320]{1,0:T(8,128)S(1)}, f32[256,320]{1,0:T(8,128)}, u32[]{:S(2)}) copy-start(f32[256,320]{1,0:T(8,128)} %fusion.39) | copy-start | bytes 983044
  582.0 2.6 copy-start.10
  615.5 0.7 copy-start.18
  616.2 63.7 %copy-start.5 = (f32[256,256]{1,0:T(8,128)S(1)}, f32[256,256]{1,0:T(8,128)}, u32[]{:S(2)}) copy-start(f32[256,256]{1,0:T(8,128)} %copy-done.4) | copy-start | bytes 786436
  651.9 2.6 copy-start.11
  688.3 0.7 copy-start.14
  740.2 11.8 %copy-start.1 = (f32[256,1024]{1,0:T(8,128)}, f32[256,1024]{1,0:T(8,128)S(1)}, u32[]{:S(2)}) copy-start(f32[256,1024]{1,0:T(8,128)S(1)} %fusion.6) | copy-start | bytes 3145732
  740.2 10.7 %copy-start.3 = (f32[256,320]{0,1:T(8,128)S(1)}, f32[256,320]{0,1:T(8,128)}, u32[]{:S(2)}) copy-start(f32[256,320]{0,1:T(8,128)} %fusion.43) | copy-start | bytes 983044
Sparse Core Ops, SparseCore 0:
  51.8 254.0 all-reduce.2
